TPU v7x, 32 devices: a whole 2x2x4 slice. The times are simulated.
32 devices in a mesh: grp: 4 (over y, core), dom: 8 (over z, x).
Axes of the slice: x: 2, y: 2, z: 4, core: 2. Of those that a mesh axis runs over, the one named last changes fastest.
Arguments:
- element_state: float32 [56, 9, 20480], P(None, None, ('grp', 'dom')), may hold values from -6 to 6
- stiffness: float32 [3, 56, 56], replicated, may hold values from -0.75 to 0.75
- flux_local: float32 [4, 56, 56], replicated, may hold values from -0.75 to 0.75
- flux_remote: float32 [4, 56, 56], replicated, may hold values from -0.75 to 0.75
- star_matrix: float32 [3, 9, 9, 20480], P(None, None, None, ('grp', 'dom')), may hold values from -0.18 to 0.18
- face_local: float32 [4, 9, 9, 20480], P(None, None, None, ('grp', 'dom')), may hold values from -0.15 to 0.15
- face_remote: float32 [4, 9, 9, 20480], P(None, None, None, ('grp', 'dom')), may hold values from -0.15 to 0.15
- energy_weight: float32 [9, 20480], P(None, ('grp', 'dom')), may hold values from 0.5 to 18
- face_neighbour: int32 [4, 20480], P(None, ('grp', 'dom')), may hold values from 0 to 1151, as said below
- element_count: int32 [32], P(('grp', 'dom')), may hold values from 160 to 640, as said below
- send_count: int32 [32, 8], P(('grp', 'dom')), may hold values from 0 to 64, as said below
- send_element: int32 [32, 8, 64], P(('grp', 'dom')), may hold values from 0 to 639, as said below
- receiver_element: int32 [512], P(('grp', 'dom')), may hold values from 0 to 639, as said below
- receiver_slot: int32 [512], P(('grp', 'dom')), may hold values from 0 to 127, as said below
- receiver_weight: float32 [56, 512], P(None, ('grp', 'dom')), may hold values from -0.75 to 0.75
Outputs:
- new_state: float32 [56, 9, 20480], P(None, None, ('grp', 'dom'))
- energy: float32 [4, 3], P('grp')
- traces: float32 [3, 9, 512], P(None, None, ('grp', 'dom'))
Inputs may be any that keep to these rules, and one draw needn't show every extreme that they name: The first element_count[p] slots of a partition are active. In every slab 4 partitions in a row along dom (cyclically) hold 640 active elements; the others hold from 160 to 320. `send_count`: every partition has exactly 64 in one of its first 6 slots. `send_element`: names active elements of the sending partition. `face_neighbour`: values below 640 name active elements of the partition itself. `receiver_element`: names an active element of the owning partition. `receiver_slot`: within each slab a permutation of the 128 rows.
All inputs are finite; a program needn't handle non-finite values.
Results may differ from a plain program's by a relative error of at most 0.0001.
Values sent between devices are 32-bit elements; how exact they have to be, the bound alone decides.
A program may use at most 128 MiB of HBM per device.

v0:
```python
import jax
import jax.numpy as jnp
from jax import lax
from jax.sharding import PartitionSpec as P

PEER_REACH = 3
TIME_STEPS = 3
highest = lax.Precision.HIGHEST


def from_behind(array, axis, by):
    count = lax.axis_size(axis)
    return lax.ppermute(array, axis, [(i, (i + by) % count) for i in range(count)])


def from_behind_2(value, axis, steps):
    count = lax.axis_size(axis)
    initial, last = (max(0, -steps), min(count, count - steps))
    return lax.ppermute(value, axis, [(source, source + steps) for source in range(initial, last)])


def element_slice(array, start, width):
    return lax.dynamic_slice_in_dim(array, start, width, array.ndim - 1)


def quantity_apply(matrices, modal_terms):
    total = None
    for column in range(matrices.shape[2]):
        term = jnp.sum(
            modal_terms[:, :, column : column + 1, :] * matrices[:, None, :, column, :], axis=0
        )
        total = term if total is None else total + term
    return total


def per_device(
    element_state,
    stiffness,
    flux_local,
    flux_remote,
    star_matrix,
    face_local,
    face_remote,
    energy_weight,
    face_neighbour,
    element_count,
    send_count,
    send_element,
    receiver_element,
    receiver_slot,
    receiver_weight,
):
    basis, quantities, elem_pad = element_state.shape
    slot_total = send_element.shape[1]
    capacity = send_element.shape[2]
    group_size = lax.axis_size("dom")
    width = min(128, elem_pad)
    live_count = element_count[0]
    live_blocks = (live_count + width - 1) // width
    stacked_local = jnp.concatenate([stiffness, flux_local], 0).reshape(-1, basis)
    local_total = stiffness.shape[0] + flux_local.shape[0]
    slot_live = jnp.arange(capacity)[None, :] < send_count[0][:, None]
    element_live = jnp.arange(elem_pad) < live_count
    denominator = float(group_size * elem_pad * basis * quantities)
    matches = (
        receiver_slot[:, None] == jnp.arange(group_size * receiver_slot.shape[0])[None, :]
    ).astype(jnp.float32)
    fields = element_state
    energies = []
    tables = []
    for time_step in range(TIME_STEPS):
        taken = jnp.take(fields, send_element[0], axis=2)
        messages = jnp.where(slot_live[None, None], taken, 0.0)

        def local_terms(block_number, partial_value):
            start = block_number * width
            block_field = element_slice(fields, start, width)
            modal_terms = jnp.dot(
                stacked_local,
                block_field.reshape(basis, -1),
                precision=highest,
                preferred_element_type=jnp.float32,
            ).reshape(local_total, basis, quantities, width)
            matrices = jnp.concatenate(
                [
                    element_slice(star_matrix, start, width),
                    -element_slice(face_local, start, width),
                ],
                0,
            )
            return lax.dynamic_update_slice_in_dim(
                partial_value, quantity_apply(matrices, modal_terms), start, 2
            )

        partial_value = lax.fori_loop(0, live_blocks, local_terms, jnp.zeros_like(fields))
        arrived = []
        for slot_number in range(2 * PEER_REACH):
            offset = slot_number + 1 if slot_number < PEER_REACH else PEER_REACH - 1 - slot_number
            arrived.append(from_behind(messages[:, :, slot_number, :], "dom", offset))
        for slot_number in range(2 * PEER_REACH, 2 * PEER_REACH + 2):
            offset = 1 if slot_number == 2 * PEER_REACH else -1
            arrived.append(from_behind_2(messages[:, :, slot_number, :], "grp", offset))
        halo_cells = jnp.stack(arrived, 2).reshape(basis, quantities, slot_total * capacity)
        extended = jnp.concatenate([fields, halo_cells], 2)

        def remote_terms(block_number, updated):
            start = block_number * width
            block_field = element_slice(fields, start, width)
            neighbours = element_slice(face_neighbour, start, width)
            nearby = jnp.take(extended, neighbours, axis=2)
            modal_terms = jnp.einsum("fbc,cqfe->fbqe", flux_remote, nearby, precision=highest)
            change = element_slice(partial_value, start, width) - quantity_apply(
                element_slice(face_remote, start, width), modal_terms
            )
            live = start + jnp.arange(width) < live_count
            renewed = jnp.where(live[None, None, :], block_field + change, block_field)
            return lax.dynamic_update_slice_in_dim(updated, renewed, start, 2)

        fields = lax.fori_loop(0, live_blocks, remote_terms, fields)
        squares = jnp.sum(fields * fields, axis=0)
        own_energy = 0.5 * jnp.sum(jnp.where(element_live[None, :], energy_weight * squares, 0.0))
        energies.append(lax.psum(own_energy, "dom") / denominator)
        values = jnp.einsum(
            "br,bqr->qr",
            receiver_weight,
            jnp.take(fields, receiver_element, axis=2),
            precision=highest,
        )
        placed = jnp.dot(values, matches, precision=highest, preferred_element_type=jnp.float32)
        tables.append(placed)
    energy = jnp.stack(energies)
    traces = lax.psum_scatter(jnp.stack(tables), "dom", scatter_dimension=2, tiled=True)
    return (fields, energy[None, :], traces)


def solution(mesh):
    return jax.shard_map(
        per_device,
        mesh=mesh,
        in_specs=(
            P(None, None, ("grp", "dom")),
            P(),
            P(),
            P(),
            P(None, None, None, ("grp", "dom")),
            P(None, None, None, ("grp", "dom")),
            P(None, None, None, ("grp", "dom")),
            P(None, ("grp", "dom")),
            P(None, ("grp", "dom")),
            P(("grp", "dom")),
            P(("grp", "dom"), None),
            P(("grp", "dom"), None, None),
            P(("grp", "dom")),
            P(("grp", "dom")),
            P(None, ("grp", "dom")),
        ),
        out_specs=(P(None, None, ("grp", "dom")), P("grp", None), P(None, None, ("grp", "dom"))),
        check_vma=False,
    )
```

profile of v0, /device:TPU:0, one launch (start us, length us, event | category | flops | bytes accessed | tf_op | source)
XLA Modules:
  0.0 804.4 jit_solution(14370141529047191707)
XLA Ops:
  40.7 36.1 %while.60 = (s32[]{:T(128)}, f32[56,9,640]{2,0,1:T(8,128)}, s32[]{:T(128)}, f32[56,9,640]{2,0,1:T(8,128)}, f32[392,56]{1,0:T(8,128)S(1)}, /*index=5*/f32[3,9,9,6...) while((s32[]{:T(128)}, f32[56,9,640]{2,0,1:T(8,128)}, ...), condition=%wide.region_10.12_spmd, body=%wide.region_0.11_spmd.sunk | while | flops 311642496 | bytes 30054112 | solution.py:95
  82.7 29.6 %collective-permute-done.1 = f32[56,9,64]{2,0,1:T(8,128)S(1)} collective-permute-done((f32[56,9,64]{2,0,1:T(8,128)S(1)}, f32[56,9,64]{2,0,1:T(8,128)S(1)}, u32[]{:S(2)}, u32[]{:S(2)}) %collective-permute-start.1) | collective-permute-done | bytes 129056 | tf_op jit(solution)/shard_map/ppermute | solution.py:13
  112.9 14.0 %collective-permute-done.2 = f32[56,9,64]{2,0,1:T(8,128)S(1)} collective-permute-done((f32[56,9,64]{2,0,1:T(8,128)S(1)}, f32[56,9,64]{2,0,1:T(8,128)S(1)}, u32[]{:S(2)}, u32[]{:S(2)}) %collective-permute-start.2) | collective-permute-done | bytes 129056 | tf_op jit(solution)/shard_map/ppermute | solution.py:13
  144.1 8.3 %copy.285 = f32[56,9,1152]{0,1,2:T(8,128)} copy(f32[56,9,1152]{2,0,1:T(8,128)} %pad_maximum_fusion.3) | data formatting | bytes 4644864 | tf_op jit(solution)/shard_map/while | solution.py:119
  152.4 51.5 %while.61 = (s32[]{:T(128)}, f32[56,9,640]{2,0,1:T(8,128)S(1)}, s32[]{:T(128)}, s32[]{:T(128)}, f32[56,9,640]{2,0,1:T(8,128)}, /*index=5*/f32[56,9,640]{2,0,1:T(...) while((s32[]{:T(128)}, f32[56,9,640]{2,0,1:T(8,128)S(1)}, ...), condition=%wide.region_21.24_spmd, body=%wide.region_11.23_spmd.sunk | while | flops 178446096 | bytes 18001700 | solution.py:119
  211.6 36.2 %while.62 = (s32[]{:T(128)}, f32[56,9,640]{2,0,1:T(8,128)}, s32[]{:T(128)}, f32[56,9,640]{2,0,1:T(8,128)S(1)}, f32[392,56]{1,0:T(8,128)S(1)}, /*index=5*/f32[3,9...) while((s32[]{:T(128)}, f32[56,9,640]{2,0,1:T(8,128)}, ...), condition=%wide.region_32.35_spmd, body=%wide.region_22.34_spmd.sunk | while | flops 311642496 | bytes 29134816 | solution.py:95
  266.9 60.5 %collective-permute-start.13 = (f32[56,9,64]{2,0,1:T(8,128)S(1)}, f32[56,9,64]{2,0,1:T(8,128)S(1)}, u32[]{:S(2)}, u32[]{:S(2)}) collective-permute-start(f32[56,9,64]{2,0,1:T(8,128)S(1)} %get-tuple-element.754), channel_id=1, source_target_pairs={{0,5},{1,6},{2,7},{3,0},{4,1},{5,2},{6,3},{7,4},{8,13},{9,14},{10,... | collective-permute-start | bytes 387080 | tf_op jit(solution)/shard_map/ppermute | solution.py:13
  330.4 15.6 %collective-permute-done.8 = f32[56,9,64]{2,0,1:T(8,128)S(1)} collective-permute-done((f32[56,9,64]{2,0,1:T(8,128)S(1)}, f32[56,9,64]{2,0,1:T(8,128)S(1)}, u32[]{:S(2)}, u32[]{:S(2)}) %collective-permute-start.8) | collective-permute-done | bytes 129056 | tf_op jit(solution)/shard_map/ppermute | solution.py:13
  347.9 8.2 %collective-permute-done.9 = f32[56,9,64]{2,0,1:T(8,128)S(1)} collective-permute-done((f32[56,9,64]{2,0,1:T(8,128)S(1)}, f32[56,9,64]{2,0,1:T(8,128)S(1)}, u32[]{:S(2)}, u32[]{:S(2)}) %collective-permute-start.9) | collective-permute-done | bytes 129056 | tf_op jit(solution)/shard_map/ppermute | solution.py:13
  356.1 13.0 %collective-permute-done.10 = f32[56,9,64]{2,0,1:T(8,128)S(1)} collective-permute-done((f32[56,9,64]{2,0,1:T(8,128)S(1)}, f32[56,9,64]{2,0,1:T(8,128)S(1)}, u32[]{:S(2)}, u32[]{:S(2)}) %collective-permute-start.10) | collective-permute-done | bytes 129056 | tf_op jit(solution)/shard_map/ppermute | solution.py:13
  369.3 8.1 %collective-permute-done.11 = f32[56,9,64]{2,0,1:T(8,128)S(1)} collective-permute-done((f32[56,9,64]{2,0,1:T(8,128)S(1)}, f32[56,9,64]{2,0,1:T(8,128)S(1)}, u32[]{:S(2)}, u32[]{:S(2)}) %collective-permute-start.11) | collective-permute-done | bytes 129056 | tf_op jit(solution)/shard_map/ppermute | solution.py:13
  382.7 8.4 %copy.293 = f32[56,9,1152]{0,1,2:T(8,128)} copy(f32[56,9,1152]{2,0,1:T(8,128)} %pad_maximum_fusion.4) | data formatting | bytes 4644864 | tf_op jit(solution)/shard_map/while | solution.py:119
  391.1 51.0 %while.63 = (s32[]{:T(128)}, f32[56,9,640]{2,0,1:T(8,128)S(1)}, s32[]{:T(128)}, s32[]{:T(128)}, f32[56,9,640]{2,0,1:T(8,128)}, /*index=5*/f32[56,9,640]{2,0,1:T(...) while((s32[]{:T(128)}, f32[56,9,640]{2,0,1:T(8,128)S(1)}, ...), condition=%wide.region_43.46_spmd, body=%wide.region_33.45_spmd.sunk | while | flops 178446096 | bytes 18001700 | solution.py:119
  457.3 36.4 %while.64 = (s32[]{:T(128)}, f32[56,9,640]{2,0,1:T(8,128)}, s32[]{:T(128)}, f32[56,9,640]{2,0,1:T(8,128)S(1)}, f32[392,56]{1,0:T(8,128)S(1)}, /*index=5*/f32[3,9...) while((s32[]{:T(128)}, f32[56,9,640]{2,0,1:T(8,128)}, ...), condition=%wide.region_54.57_spmd, body=%wide.region_44.56_spmd.sunk | while | flops 311642496 | bytes 29134816 | solution.py:95
  506.3 61.6 %collective-permute-start.21 = (f32[56,9,64]{2,0,1:T(8,128)S(1)}, f32[56,9,64]{2,0,1:T(8,128)S(1)}, u32[]{:S(2)}, u32[]{:S(2)}) collective-permute-start(f32[56,9,64]{2,0,1:T(8,128)S(1)} %get-tuple-element.746), channel_id=1, source_target_pairs={{0,5},{1,6},{2,7},{3,0},{4,1},{5,2},{6,3},{7,4},{8,13},{9,14},{10,... | collective-permute-start | bytes 387080 | tf_op jit(solution)/shard_map/ppermute | solution.py:13
  570.2 15.8 %collective-permute-done.17 = f32[56,9,64]{2,0,1:T(8,128)S(1)} collective-permute-done((f32[56,9,64]{2,0,1:T(8,128)S(1)}, f32[56,9,64]{2,0,1:T(8,128)S(1)}, u32[]{:S(2)}, u32[]{:S(2)}) %collective-permute-start.17) | collective-permute-done | bytes 129056 | tf_op jit(solution)/shard_map/ppermute | solution.py:13
  588.6 12.8 %collective-permute-done.18 = f32[56,9,64]{2,0,1:T(8,128)S(1)} collective-permute-done((f32[56,9,64]{2,0,1:T(8,128)S(1)}, f32[56,9,64]{2,0,1:T(8,128)S(1)}, u32[]{:S(2)}, u32[]{:S(2)}) %collective-permute-start.18) | collective-permute-done | bytes 129056 | tf_op jit(solution)/shard_map/ppermute | solution.py:13
  601.4 7.1 collective-permute-done.19
  613.8 8.3 %copy.307 = f32[56,9,1152]{0,1,2:T(8,128)} copy(f32[56,9,1152]{2,0,1:T(8,128)} %pad_maximum_fusion.5) | data formatting | bytes 4644864 | tf_op jit(solution)/shard_map/while | solution.py:119
  622.1 47.4 %while.65 = (s32[]{:T(128)}, f32[56,9,640]{2,0,1:T(8,128)}, s32[]{:T(128)}, s32[]{:T(128)}, f32[56,9,640]{2,0,1:T(8,128)S(1)}, /*index=5*/f32[56,9,640]{2,0,1:T(...) while((s32[]{:T(128)}, f32[56,9,640]{2,0,1:T(8,128)}, ...), condition=%wide.region_65.68_spmd, body=%wide.region_55.67_spmd.sunk | while | flops 178446096 | bytes 17336972 | solution.py:119
  623.8 6.7 gather_fusion.2
  639.6 6.7 gather_fusion.2
  678.5 52.2 %all-reduce = (f32[]{:T(128)}, f32[]{:T(128)}, f32[]{:T(128)}) all-reduce(f32[]{:T(128)S(6)} %mul.971, f32[]{:T(128)S(6)} %mul.968, f32[]{:T(128)S(6)} %mul.965), channel_id=1, replica_groups=mesh['grp'=4,'dom'=8] {'dom'}, use_global_device_ids=true, to_apply=%region_74.77 | all-reduce | flops 3 | bytes 24 | tf_op jit(solution)/shard_map/psum | solution.py:122
  738.0 57.9 %reduce-scatter.4.cloned.1.call-done = f32[16,27]{1,0:T(8,128)} async-done(((f32[128,27]{1,0:T(8,128)}), f32[16,27]{1,0:T(8,128)}) %reduce-scatter.4.cloned.1.call-update) | async-done | bytes 1744
  (748 shorter events, 386.1 us)
Async XLA Ops:
  7.2 788.7 %reduce-scatter.4.cloned.1.call-start = ((), (), s32[]{:S(2)}) async-start(), calls=%async_computation.1 | async-start | bytes 73728
  25.4 111.2 %collective-permute-start.7 = (f32[56,9,64]{2,0,1:T(8,128)}, f32[56,9,64]{2,0,1:T(8,128)}, u32[]{:S(2)}, u32[]{:S(2)}) collective-permute-start(f32[56,9,64]{2,0,1:T(8,128)} %get-tuple-element.760), channel_id=1, source_target_pairs={{8,0},{16,8},{24,16},{9,1},{17,9},{25,17},{10,2},{18,10},{26,18},{... | collective-permute-start | bytes 387080 | tf_op jit(solution)/shard_map/ppermute | solution.py:19
  26.7 109.0 %collective-permute-start.6 = (f32[56,9,64]{2,0,1:T(8,128)}, f32[56,9,64]{2,0,1:T(8,128)}, u32[]{:S(2)}, u32[]{:S(2)}) collective-permute-start(f32[56,9,64]{2,0,1:T(8,128)} %get-tuple-element.761), channel_id=1, source_target_pairs={{0,8},{8,16},{16,24},{1,9},{9,17},{17,25},{2,10},{10,18},{18,26},{... | collective-permute-start | bytes 387080 | tf_op jit(solution)/shard_map/ppermute | solution.py:19
  30.4 104.2 %collective-permute-start.5 = (f32[56,9,64]{2,0,1:T(8,128)}, f32[56,9,64]{2,0,1:T(8,128)}, u32[]{:S(2)}, u32[]{:S(2)}) collective-permute-start(f32[56,9,64]{2,0,1:T(8,128)} %get-tuple-element.762), channel_id=1, source_target_pairs={{0,5},{1,6},{2,7},{3,0},{4,1},{5,2},{6,3},{7,4},{8,13},{9,14},{10,... | collective-permute-start | bytes 387080 | tf_op jit(solution)/shard_map/ppermute | solution.py:13
  35.4 98.3 %collective-permute-start.4 = (f32[56,9,64]{2,0,1:T(8,128)}, f32[56,9,64]{2,0,1:T(8,128)}, u32[]{:S(2)}, u32[]{:S(2)}) collective-permute-start(f32[56,9,64]{2,0,1:T(8,128)} %get-tuple-element.763), channel_id=1, source_target_pairs={{0,6},{1,7},{2,0},{3,1},{4,2},{5,3},{6,4},{7,5},{8,14},{9,15},{10,... | collective-permute-start | bytes 387080 | tf_op jit(solution)/shard_map/ppermute | solution.py:13
  36.8 44.9 %collective-permute-start = (f32[56,9,64]{2,0,1:T(8,128)}, f32[56,9,64]{2,0,1:T(8,128)}, u32[]{:S(2)}, u32[]{:S(2)}) collective-permute-start(f32[56,9,64]{2,0,1:T(8,128)} %get-tuple-element.767), channel_id=1, source_target_pairs={{0,1},{1,2},{2,3},{3,4},{4,5},{5,6},{6,7},{7,0},{8,9},{9,10},{10,1... | collective-permute-start | bytes 387080 | tf_op jit(solution)/shard_map/ppermute | solution.py:13
  81.7 30.5 %collective-permute-start.1 = (f32[56,9,64]{2,0,1:T(8,128)S(1)}, f32[56,9,64]{2,0,1:T(8,128)S(1)}, u32[]{:S(2)}, u32[]{:S(2)}) collective-permute-start(f32[56,9,64]{2,0,1:T(8,128)S(1)} %copy-done.63), channel_id=1, source_target_pairs={{0,2},{1,3},{2,4},{3,5},{4,6},{5,7},{6,0},{7,1},{8,10},{9,11},{10,... | collective-permute-start | bytes 387080 | tf_op jit(solution)/shard_map/ppermute | solution.py:13
  112.2 14.7 %collective-permute-start.2 = (f32[56,9,64]{2,0,1:T(8,128)S(1)}, f32[56,9,64]{2,0,1:T(8,128)S(1)}, u32[]{:S(2)}, u32[]{:S(2)}) collective-permute-start(f32[56,9,64]{2,0,1:T(8,128)S(1)} %copy-done.62), channel_id=1, source_target_pairs={{0,3},{1,4},{2,5},{3,6},{4,7},{5,0},{6,1},{7,2},{8,11},{9,12},{10,... | collective-permute-start | bytes 387080 | tf_op jit(solution)/shard_map/ppermute | solution.py:13
  262.5 115.0 %collective-permute-start.15 = (f32[56,9,64]{2,0,1:T(8,128)S(1)}, f32[56,9,64]{2,0,1:T(8,128)S(1)}, u32[]{:S(2)}, u32[]{:S(2)}) collective-permute-start(f32[56,9,64]{2,0,1:T(8,128)S(1)} %get-tuple-element.752), channel_id=1, source_target_pairs={{8,0},{16,8},{24,16},{9,1},{17,9},{25,17},{10,2},{18,10},{26,18},{... | collective-permute-start | bytes 387080 | tf_op jit(solution)/shard_map/ppermute | solution.py:19
  263.8 113.6 %collective-permute-start.14 = (f32[56,9,64]{2,0,1:T(8,128)S(1)}, f32[56,9,64]{2,0,1:T(8,128)S(1)}, u32[]{:S(2)}, u32[]{:S(2)}) collective-permute-start(f32[56,9,64]{2,0,1:T(8,128)S(1)} %get-tuple-element.753), channel_id=1, source_target_pairs={{0,8},{8,16},{16,24},{1,9},{9,17},{17,25},{2,10},{10,18},{18,26},{... | collective-permute-start | bytes 387080 | tf_op jit(solution)/shard_map/ppermute | solution.py:19
  266.9 110.5 %collective-permute-start.13 = (f32[56,9,64]{2,0,1:T(8,128)S(1)}, f32[56,9,64]{2,0,1:T(8,128)S(1)}, u32[]{:S(2)}, u32[]{:S(2)}) collective-permute-start(f32[56,9,64]{2,0,1:T(8,128)S(1)} %get-tuple-element.754), channel_id=1, source_target_pairs={{0,5},{1,6},{2,7},{3,0},{4,1},{5,2},{6,3},{7,4},{8,13},{9,14},{10,... | collective-permute-start | bytes 387080 | tf_op jit(solution)/shard_map/ppermute | solution.py:13
  327.4 50.0 %collective-permute-start.12 = (f32[56,9,64]{2,0,1:T(8,128)S(1)}, f32[56,9,64]{2,0,1:T(8,128)S(1)}, u32[]{:S(2)}, u32[]{:S(2)}) collective-permute-start(f32[56,9,64]{2,0,1:T(8,128)S(1)} %get-tuple-element.755), channel_id=1, source_target_pairs={{0,6},{1,7},{2,0},{3,1},{4,2},{5,3},{6,4},{7,5},{8,14},{9,15},{10,... | collective-permute-start | bytes 387080 | tf_op jit(solution)/shard_map/ppermute | solution.py:13
  327.8 18.2 %collective-permute-start.8 = (f32[56,9,64]{2,0,1:T(8,128)S(1)}, f32[56,9,64]{2,0,1:T(8,128)S(1)}, u32[]{:S(2)}, u32[]{:S(2)}) collective-permute-start(f32[56,9,64]{2,0,1:T(8,128)S(1)} %get-tuple-element.759), channel_id=1, source_target_pairs={{0,1},{1,2},{2,3},{3,4},{4,5},{5,6},{6,7},{7,0},{8,9},{9,10},{10,1... | collective-permute-start | bytes 387080 | tf_op jit(solution)/shard_map/ppermute | solution.py:13
  346.0 10.0 %collective-permute-start.9 = (f32[56,9,64]{2,0,1:T(8,128)S(1)}, f32[56,9,64]{2,0,1:T(8,128)S(1)}, u32[]{:S(2)}, u32[]{:S(2)}) collective-permute-start(f32[56,9,64]{2,0,1:T(8,128)S(1)} %get-tuple-element.758), channel_id=1, source_target_pairs={{0,2},{1,3},{2,4},{3,5},{4,6},{5,7},{6,0},{7,1},{8,10},{9,11},{10,... | collective-permute-start | bytes 387080 | tf_op jit(solution)/shard_map/ppermute | solution.py:13
  356.0 13.0 %collective-permute-start.10 = (f32[56,9,64]{2,0,1:T(8,128)S(1)}, f32[56,9,64]{2,0,1:T(8,128)S(1)}, u32[]{:S(2)}, u32[]{:S(2)}) collective-permute-start(f32[56,9,64]{2,0,1:T(8,128)S(1)} %get-tuple-element.757), channel_id=1, source_target_pairs={{0,3},{1,4},{2,5},{3,6},{4,7},{5,0},{6,1},{7,2},{8,11},{9,12},{10,... | collective-permute-start | bytes 387080 | tf_op jit(solution)/shard_map/ppermute | solution.py:13
  369.1 8.3 %collective-permute-start.11 = (f32[56,9,64]{2,0,1:T(8,128)S(1)}, f32[56,9,64]{2,0,1:T(8,128)S(1)}, u32[]{:S(2)}, u32[]{:S(2)}) collective-permute-start(f32[56,9,64]{2,0,1:T(8,128)S(1)} %get-tuple-element.756), channel_id=1, source_target_pairs={{0,7},{1,0},{2,1},{3,2},{4,3},{5,4},{6,5},{7,6},{8,15},{9,8},{10,9... | collective-permute-start | bytes 387080 | tf_op jit(solution)/shard_map/ppermute | solution.py:13
  500.7 67.6 %collective-permute-start.16 = (f32[56,9,64]{2,0,1:T(8,128)S(1)}, f32[56,9,64]{2,0,1:T(8,128)S(1)}, u32[]{:S(2)}, u32[]{:S(2)}) collective-permute-start(f32[56,9,64]{2,0,1:T(8,128)S(1)} %get-tuple-element.751), channel_id=1, source_target_pairs={{0,1},{1,2},{2,3},{3,4},{4,5},{5,6},{6,7},{7,0},{8,9},{9,10},{10,1... | collective-permute-start | bytes 387080 | tf_op jit(solution)/shard_map/ppermute | solution.py:13
  501.9 106.7 %collective-permute-start.23 = (f32[56,9,64]{2,0,1:T(8,128)S(1)}, f32[56,9,64]{2,0,1:T(8,128)S(1)}, u32[]{:S(2)}, u32[]{:S(2)}) collective-permute-start(f32[56,9,64]{2,0,1:T(8,128)S(1)} %get-tuple-element.744), channel_id=1, source_target_pairs={{8,0},{16,8},{24,16},{9,1},{17,9},{25,17},{10,2},{18,10},{26,18},{... | collective-permute-start | bytes 387080 | tf_op jit(solution)/shard_map/ppermute | solution.py:19
  503.2 105.4 %collective-permute-start.22 = (f32[56,9,64]{2,0,1:T(8,128)S(1)}, f32[56,9,64]{2,0,1:T(8,128)S(1)}, u32[]{:S(2)}, u32[]{:S(2)}) collective-permute-start(f32[56,9,64]{2,0,1:T(8,128)S(1)} %get-tuple-element.745), channel_id=1, source_target_pairs={{0,8},{8,16},{16,24},{1,9},{9,17},{17,25},{2,10},{10,18},{18,26},{... | collective-permute-start | bytes 387080 | tf_op jit(solution)/shard_map/ppermute | solution.py:19
  506.3 102.3 %collective-permute-start.21 = (f32[56,9,64]{2,0,1:T(8,128)S(1)}, f32[56,9,64]{2,0,1:T(8,128)S(1)}, u32[]{:S(2)}, u32[]{:S(2)}) collective-permute-start(f32[56,9,64]{2,0,1:T(8,128)S(1)} %get-tuple-element.746), channel_id=1, source_target_pairs={{0,5},{1,6},{2,7},{3,0},{4,1},{5,2},{6,3},{7,4},{8,13},{9,14},{10,... | collective-permute-start | bytes 387080 | tf_op jit(solution)/shard_map/ppermute | solution.py:13
  567.9 40.6 %collective-permute-start.20 = (f32[56,9,64]{2,0,1:T(8,128)S(1)}, f32[56,9,64]{2,0,1:T(8,128)S(1)}, u32[]{:S(2)}, u32[]{:S(2)}) collective-permute-start(f32[56,9,64]{2,0,1:T(8,128)S(1)} %get-tuple-element.747), channel_id=1, source_target_pairs={{0,6},{1,7},{2,0},{3,1},{4,2},{5,3},{6,4},{7,5},{8,14},{9,15},{10,... | collective-permute-start | bytes 387080 | tf_op jit(solution)/shard_map/ppermute | solution.py:13
  568.3 17.7 %collective-permute-start.17 = (f32[56,9,64]{2,0,1:T(8,128)S(1)}, f32[56,9,64]{2,0,1:T(8,128)S(1)}, u32[]{:S(2)}, u32[]{:S(2)}) collective-permute-start(f32[56,9,64]{2,0,1:T(8,128)S(1)} %get-tuple-element.750), channel_id=1, source_target_pairs={{0,2},{1,3},{2,4},{3,5},{4,6},{5,7},{6,0},{7,1},{8,10},{9,11},{10,... | collective-permute-start | bytes 387080 | tf_op jit(solution)/shard_map/ppermute | solution.py:13
  586.0 15.3 %collective-permute-start.18 = (f32[56,9,64]{2,0,1:T(8,128)S(1)}, f32[56,9,64]{2,0,1:T(8,128)S(1)}, u32[]{:S(2)}, u32[]{:S(2)}) collective-permute-start(f32[56,9,64]{2,0,1:T(8,128)S(1)} %get-tuple-element.749), channel_id=1, source_target_pairs={{0,3},{1,4},{2,5},{3,6},{4,7},{5,0},{6,1},{7,2},{8,11},{9,12},{10,... | collective-permute-start | bytes 387080 | tf_op jit(solution)/shard_map/ppermute | solution.py:13
  601.3 7.1 collective-permute-start.19
  (188 other events, 1366.5 us)
Sparse Core Ops, SparseCore 0:
  737.5 58.3 reduce-scatter.3
where the time goes:
time: 819 us; the launch traced here: 804 us
  local copies, waits for them, and re-layouts  262 us (32%)
  waiting for transfers between devices  189 us (23%)
  starting transfers between devices  152 us (19%)
  other arithmetic  83.2 us (10%)
  blocking collectives  52.2 us (6%)
  matrix products  42.8 us (5%)
  between operations  19.4 us (2%)
    ppermute x18, starting transfers between devices, from_behind(): lax.ppermute(array, axis, [(i, (i + by) % count) for i in range(count)])  138 us
    ppermute x18, waiting for transfers between devices, from_behind(): lax.ppermute(array, axis, [(i, (i + by) % count) for i in range(count)])  131 us
    gather x18, local copies, waits for them, and re-layouts, remote_terms(): nearby = jnp.take(extended, neighbours, axis=2)  90.2 us
    unnamed x2, waiting for transfers between devices  57.9 us
    psum x1, blocking collectives, per_device(): energies.append(lax.psum(own_energy, 'dom') / denominator)  52.2 us
    while x7, local copies, waits for them, and re-layouts, per_device(): fields = lax.fori_loop(0, live_blocks, remote_terms, fields)  40.5 us
    dot_general x9, matrix products, local_terms(): jnp.dot(stacked_local, block_field.reshape(basis, -1), precision=highest,...  29.6 us
    gather x6, local copies, waits for them, and re-layouts, per_device(): taken = jnp.take(fields, send_element[0], axis=2)  26.9 us
  transfers between devices with their start and end apart: 25, of which 11 were waited for; matrix products, arithmetic and copies ran while one was open for 6% of the time, Pallas kernels for 0%

commit v1 on v0

--- a/solution.py
+++ b/solution.py
@@ -6,6 +6,10 @@
 PEER_REACH = 3
 TIME_STEPS = 3
 highest = lax.Precision.HIGHEST
+
+
+def begin_series_all(z, row_axis="dom"):
+    return lax.all_gather(z, row_axis).sum(axis=0)
 
 
 def from_behind(array, axis, by):
@@ -119,7 +123,7 @@
         fields = lax.fori_loop(0, live_blocks, remote_terms, fields)
         squares = jnp.sum(fields * fields, axis=0)
         own_energy = 0.5 * jnp.sum(jnp.where(element_live[None, :], energy_weight * squares, 0.0))
-        energies.append(lax.psum(own_energy, "dom") / denominator)
+        energies.append(begin_series_all(own_energy) / denominator)
         values = jnp.einsum(
             "br,bqr->qr",
             receiver_weight,

time: 819 us -> 823 us (level)
    psum x1 -> x0, blocking collectives: 52.2 us -> none  [per_device(): energies.append(lax.psum(own_energy, 'dom') / denominator)]
    unnamed x0 -> x1, blocking collectives: none -> 51.6 us
    unnamed x85 -> x94, local copies, waits for them, and re-layouts: 16.9 us -> 19.5 us
where the time goes in v1:
time: 823 us; the launch traced here: 808 us
  local copies, waits for them, and re-layouts  265 us (32%)
  waiting for transfers between devices  189 us (23%)
  starting transfers between devices  152 us (18%)
  other arithmetic  85 us (10%)
  blocking collectives  51.6 us (6%)
  matrix products  42.8 us (5%)
  between operations  19.5 us (2%)
    ppermute x18, starting transfers between devices, from_behind(): lax.ppermute(array, axis, [(i, (i + by) % count) for i in range(count)])  138 us
    ppermute x18, waiting for transfers between devices, from_behind(): lax.ppermute(array, axis, [(i, (i + by) % count) for i in range(count)])  131 us
    gather x18, local copies, waits for them, and re-layouts, remote_terms(): nearby = jnp.take(extended, neighbours, axis=2)  90.2 us
    unnamed x2, waiting for transfers between devices  57.9 us
    unnamed x1, blocking collectives  51.6 us
    while x7, local copies, waits for them, and re-layouts, per_device(): fields = lax.fori_loop(0, live_blocks, remote_terms, fields)  40.5 us
    dot_general x9, matrix products, local_terms(): jnp.dot(stacked_local, block_field.reshape(basis, -1), precision=highest,...  29.6 us
    gather x6, local copies, waits for them, and re-layouts, per_device(): taken = jnp.take(fields, send_element[0], axis=2)  26.9 us
  transfers between devices with their start and end apart: 25, of which 11 were waited for; matrix products, arithmetic and copies ran while one was open for 6% of the time, Pallas kernels for 0%

profile of v1, /device:TPU:0, one launch (start us, length us, event | category | flops | bytes accessed | tf_op | source)
XLA Modules:
  0.0 808.3 jit_solution(16460552303858930530)
XLA Ops:
  40.7 36.1 %while.60 = (s32[]{:T(128)}, f32[56,9,640]{2,0,1:T(8,128)}, s32[]{:T(128)}, f32[56,9,640]{2,0,1:T(8,128)}, f32[392,56]{1,0:T(8,128)S(1)}, /*index=5*/f32[3,9,9,6...) while((s32[]{:T(128)}, f32[56,9,640]{2,0,1:T(8,128)}, ...), condition=%wide.region_10.12_spmd, body=%wide.region_0.11_spmd.sunk | while | flops 311642496 | bytes 30054112 | solution.py:99
  83.2 29.6 %collective-permute-done.1 = f32[56,9,64]{2,0,1:T(8,128)S(1)} collective-permute-done((f32[56,9,64]{2,0,1:T(8,128)S(1)}, f32[56,9,64]{2,0,1:T(8,128)S(1)}, u32[]{:S(2)}, u32[]{:S(2)}) %collective-permute-start.1) | collective-permute-done | bytes 129056 | tf_op jit(solution)/shard_map/ppermute | solution.py:17
  113.4 14.0 %collective-permute-done.2 = f32[56,9,64]{2,0,1:T(8,128)S(1)} collective-permute-done((f32[56,9,64]{2,0,1:T(8,128)S(1)}, f32[56,9,64]{2,0,1:T(8,128)S(1)}, u32[]{:S(2)}, u32[]{:S(2)}) %collective-permute-start.2) | collective-permute-done | bytes 129056 | tf_op jit(solution)/shard_map/ppermute | solution.py:17
  144.6 8.3 %copy.285 = f32[56,9,1152]{0,1,2:T(8,128)} copy(f32[56,9,1152]{2,0,1:T(8,128)} %pad_maximum_fusion.3) | data formatting | bytes 4644864 | tf_op jit(solution)/shard_map/while | solution.py:123
  153.0 51.5 %while.61 = (s32[]{:T(128)}, f32[56,9,640]{2,0,1:T(8,128)S(1)}, s32[]{:T(128)}, s32[]{:T(128)}, f32[56,9,640]{2,0,1:T(8,128)}, /*index=5*/f32[56,9,640]{2,0,1:T(...) while((s32[]{:T(128)}, f32[56,9,640]{2,0,1:T(8,128)S(1)}, ...), condition=%wide.region_21.24_spmd, body=%wide.region_11.23_spmd.sunk | while | flops 178446096 | bytes 18001700 | solution.py:123
  212.1 36.3 %while.62 = (s32[]{:T(128)}, f32[56,9,640]{2,0,1:T(8,128)}, s32[]{:T(128)}, f32[56,9,640]{2,0,1:T(8,128)S(1)}, f32[392,56]{1,0:T(8,128)S(1)}, /*index=5*/f32[3,9...) while((s32[]{:T(128)}, f32[56,9,640]{2,0,1:T(8,128)}, ...), condition=%wide.region_32.35_spmd, body=%wide.region_22.34_spmd.sunk | while | flops 311642496 | bytes 29134816 | solution.py:99
  267.5 60.5 %collective-permute-start.13 = (f32[56,9,64]{2,0,1:T(8,128)S(1)}, f32[56,9,64]{2,0,1:T(8,128)S(1)}, u32[]{:S(2)}, u32[]{:S(2)}) collective-permute-start(f32[56,9,64]{2,0,1:T(8,128)S(1)} %get-tuple-element.754), channel_id=1, source_target_pairs={{0,5},{1,6},{2,7},{3,0},{4,1},{5,2},{6,3},{7,4},{8,13},{9,14},{10,... | collective-permute-start | bytes 387080 | tf_op jit(solution)/shard_map/ppermute | solution.py:17
  330.9 15.6 %collective-permute-done.8 = f32[56,9,64]{2,0,1:T(8,128)S(1)} collective-permute-done((f32[56,9,64]{2,0,1:T(8,128)S(1)}, f32[56,9,64]{2,0,1:T(8,128)S(1)}, u32[]{:S(2)}, u32[]{:S(2)}) %collective-permute-start.8) | collective-permute-done | bytes 129056 | tf_op jit(solution)/shard_map/ppermute | solution.py:17
  348.4 8.2 %collective-permute-done.9 = f32[56,9,64]{2,0,1:T(8,128)S(1)} collective-permute-done((f32[56,9,64]{2,0,1:T(8,128)S(1)}, f32[56,9,64]{2,0,1:T(8,128)S(1)}, u32[]{:S(2)}, u32[]{:S(2)}) %collective-permute-start.9) | collective-permute-done | bytes 129056 | tf_op jit(solution)/shard_map/ppermute | solution.py:17
  356.6 13.0 %collective-permute-done.10 = f32[56,9,64]{2,0,1:T(8,128)S(1)} collective-permute-done((f32[56,9,64]{2,0,1:T(8,128)S(1)}, f32[56,9,64]{2,0,1:T(8,128)S(1)}, u32[]{:S(2)}, u32[]{:S(2)}) %collective-permute-start.10) | collective-permute-done | bytes 129056 | tf_op jit(solution)/shard_map/ppermute | solution.py:17
  369.8 8.1 %collective-permute-done.11 = f32[56,9,64]{2,0,1:T(8,128)S(1)} collective-permute-done((f32[56,9,64]{2,0,1:T(8,128)S(1)}, f32[56,9,64]{2,0,1:T(8,128)S(1)}, u32[]{:S(2)}, u32[]{:S(2)}) %collective-permute-start.11) | collective-permute-done | bytes 129056 | tf_op jit(solution)/shard_map/ppermute | solution.py:17
  383.2 8.4 %copy.293 = f32[56,9,1152]{0,1,2:T(8,128)} copy(f32[56,9,1152]{2,0,1:T(8,128)} %pad_maximum_fusion.4) | data formatting | bytes 4644864 | tf_op jit(solution)/shard_map/while | solution.py:123
  391.7 51.0 %while.63 = (s32[]{:T(128)}, f32[56,9,640]{2,0,1:T(8,128)S(1)}, s32[]{:T(128)}, s32[]{:T(128)}, f32[56,9,640]{2,0,1:T(8,128)}, /*index=5*/f32[56,9,640]{2,0,1:T(...) while((s32[]{:T(128)}, f32[56,9,640]{2,0,1:T(8,128)S(1)}, ...), condition=%wide.region_43.46_spmd, body=%wide.region_33.45_spmd.sunk | while | flops 178446096 | bytes 18001700 | solution.py:123
  457.8 36.4 %while.64 = (s32[]{:T(128)}, f32[56,9,640]{2,0,1:T(8,128)}, s32[]{:T(128)}, f32[56,9,640]{2,0,1:T(8,128)S(1)}, f32[392,56]{1,0:T(8,128)S(1)}, /*index=5*/f32[3,9...) while((s32[]{:T(128)}, f32[56,9,640]{2,0,1:T(8,128)}, ...), condition=%wide.region_54.57_spmd, body=%wide.region_44.56_spmd.sunk | while | flops 311642496 | bytes 29134816 | solution.py:99
  506.8 61.6 %collective-permute-start.21 = (f32[56,9,64]{2,0,1:T(8,128)S(1)}, f32[56,9,64]{2,0,1:T(8,128)S(1)}, u32[]{:S(2)}, u32[]{:S(2)}) collective-permute-start(f32[56,9,64]{2,0,1:T(8,128)S(1)} %get-tuple-element.746), channel_id=1, source_target_pairs={{0,5},{1,6},{2,7},{3,0},{4,1},{5,2},{6,3},{7,4},{8,13},{9,14},{10,... | collective-permute-start | bytes 387080 | tf_op jit(solution)/shard_map/ppermute | solution.py:17
  570.7 15.8 %collective-permute-done.17 = f32[56,9,64]{2,0,1:T(8,128)S(1)} collective-permute-done((f32[56,9,64]{2,0,1:T(8,128)S(1)}, f32[56,9,64]{2,0,1:T(8,128)S(1)}, u32[]{:S(2)}, u32[]{:S(2)}) %collective-permute-start.17) | collective-permute-done | bytes 129056 | tf_op jit(solution)/shard_map/ppermute | solution.py:17
  589.1 12.8 %collective-permute-done.18 = f32[56,9,64]{2,0,1:T(8,128)S(1)} collective-permute-done((f32[56,9,64]{2,0,1:T(8,128)S(1)}, f32[56,9,64]{2,0,1:T(8,128)S(1)}, u32[]{:S(2)}, u32[]{:S(2)}) %collective-permute-start.18) | collective-permute-done | bytes 129056 | tf_op jit(solution)/shard_map/ppermute | solution.py:17
  602.0 7.1 collective-permute-done.19
  614.4 8.3 %copy.307 = f32[56,9,1152]{0,1,2:T(8,128)} copy(f32[56,9,1152]{2,0,1:T(8,128)} %pad_maximum_fusion.5) | data formatting | bytes 4644864 | tf_op jit(solution)/shard_map/while | solution.py:123
  622.7 47.4 %while.65 = (s32[]{:T(128)}, f32[56,9,640]{2,0,1:T(8,128)}, s32[]{:T(128)}, s32[]{:T(128)}, f32[56,9,640]{2,0,1:T(8,128)S(1)}, /*index=5*/f32[56,9,640]{2,0,1:T(...) while((s32[]{:T(128)}, f32[56,9,640]{2,0,1:T(8,128)}, ...), condition=%wide.region_65.68_spmd, body=%wide.region_55.67_spmd.sunk | while | flops 178446096 | bytes 17336972 | solution.py:123
  624.4 6.7 gather_fusion.2
  640.1 6.7 gather_fusion.2
  681.0 51.6 %all-reduce.3 = (f32[8]{0:T(128)S(1)}, f32[8]{0:T(128)S(1)}, f32[8]{0:T(128)S(1)}) all-reduce(f32[8]{0:T(128)S(1)} %dynamic-update-slice.2, f32[8]{0:T(128)S(1)} %dynamic-update-slice.1, f32[8]{0:T(128)S(1)} %dynamic-update-slice), channel_id=1, replica_groups=mesh['grp'=4,'dom'=8] {'dom'}, use_global_device_ids=true, to_apply=%add.2 | all-reduce | flops 24 | bytes 192
  741.8 57.9 %reduce-scatter.4.cloned.1.call-done = f32[16,27]{1,0:T(8,128)} async-done(((f32[128,27]{1,0:T(8,128)}), f32[16,27]{1,0:T(8,128)}) %reduce-scatter.4.cloned.1.call-update) | async-done | bytes 1744
  (760 shorter events, 390.4 us)
Async XLA Ops:
  7.2 792.5 %reduce-scatter.4.cloned.1.call-start = ((), (), s32[]{:S(2)}) async-start(), calls=%async_computation.1 | async-start | bytes 73728
  25.4 111.8 %collective-permute-start.7 = (f32[56,9,64]{2,0,1:T(8,128)}, f32[56,9,64]{2,0,1:T(8,128)}, u32[]{:S(2)}, u32[]{:S(2)}) collective-permute-start(f32[56,9,64]{2,0,1:T(8,128)} %get-tuple-element.760), channel_id=1, source_target_pairs={{8,0},{16,8},{24,16},{9,1},{17,9},{25,17},{10,2},{18,10},{26,18},{... | collective-permute-start | bytes 387080 | tf_op jit(solution)/shard_map/ppermute | solution.py:23
  26.7 109.5 %collective-permute-start.6 = (f32[56,9,64]{2,0,1:T(8,128)}, f32[56,9,64]{2,0,1:T(8,128)}, u32[]{:S(2)}, u32[]{:S(2)}) collective-permute-start(f32[56,9,64]{2,0,1:T(8,128)} %get-tuple-element.761), channel_id=1, source_target_pairs={{0,8},{8,16},{16,24},{1,9},{9,17},{17,25},{2,10},{10,18},{18,26},{... | collective-permute-start | bytes 387080 | tf_op jit(solution)/shard_map/ppermute | solution.py:23
  30.4 104.8 %collective-permute-start.5 = (f32[56,9,64]{2,0,1:T(8,128)}, f32[56,9,64]{2,0,1:T(8,128)}, u32[]{:S(2)}, u32[]{:S(2)}) collective-permute-start(f32[56,9,64]{2,0,1:T(8,128)} %get-tuple-element.762), channel_id=1, source_target_pairs={{0,5},{1,6},{2,7},{3,0},{4,1},{5,2},{6,3},{7,4},{8,13},{9,14},{10,... | collective-permute-start | bytes 387080 | tf_op jit(solution)/shard_map/ppermute | solution.py:17
  35.4 98.8 %collective-permute-start.4 = (f32[56,9,64]{2,0,1:T(8,128)}, f32[56,9,64]{2,0,1:T(8,128)}, u32[]{:S(2)}, u32[]{:S(2)}) collective-permute-start(f32[56,9,64]{2,0,1:T(8,128)} %get-tuple-element.763), channel_id=1, source_target_pairs={{0,6},{1,7},{2,0},{3,1},{4,2},{5,3},{6,4},{7,5},{8,14},{9,15},{10,... | collective-permute-start | bytes 387080 | tf_op jit(solution)/shard_map/ppermute | solution.py:17
  36.8 45.5 %collective-permute-start = (f32[56,9,64]{2,0,1:T(8,128)}, f32[56,9,64]{2,0,1:T(8,128)}, u32[]{:S(2)}, u32[]{:S(2)}) collective-permute-start(f32[56,9,64]{2,0,1:T(8,128)} %get-tuple-element.767), channel_id=1, source_target_pairs={{0,1},{1,2},{2,3},{3,4},{4,5},{5,6},{6,7},{7,0},{8,9},{9,10},{10,1... | collective-permute-start | bytes 387080 | tf_op jit(solution)/shard_map/ppermute | solution.py:17
  82.2 30.5 %collective-permute-start.1 = (f32[56,9,64]{2,0,1:T(8,128)S(1)}, f32[56,9,64]{2,0,1:T(8,128)S(1)}, u32[]{:S(2)}, u32[]{:S(2)}) collective-permute-start(f32[56,9,64]{2,0,1:T(8,128)S(1)} %copy-done.63), channel_id=1, source_target_pairs={{0,2},{1,3},{2,4},{3,5},{4,6},{5,7},{6,0},{7,1},{8,10},{9,11},{10,... | collective-permute-start | bytes 387080 | tf_op jit(solution)/shard_map/ppermute | solution.py:17
  112.8 14.7 %collective-permute-start.2 = (f32[56,9,64]{2,0,1:T(8,128)S(1)}, f32[56,9,64]{2,0,1:T(8,128)S(1)}, u32[]{:S(2)}, u32[]{:S(2)}) collective-permute-start(f32[56,9,64]{2,0,1:T(8,128)S(1)} %copy-done.62), channel_id=1, source_target_pairs={{0,3},{1,4},{2,5},{3,6},{4,7},{5,0},{6,1},{7,2},{8,11},{9,12},{10,... | collective-permute-start | bytes 387080 | tf_op jit(solution)/shard_map/ppermute | solution.py:17
  263.1 114.9 %collective-permute-start.15 = (f32[56,9,64]{2,0,1:T(8,128)S(1)}, f32[56,9,64]{2,0,1:T(8,128)S(1)}, u32[]{:S(2)}, u32[]{:S(2)}) collective-permute-start(f32[56,9,64]{2,0,1:T(8,128)S(1)} %get-tuple-element.752), channel_id=1, source_target_pairs={{8,0},{16,8},{24,16},{9,1},{17,9},{25,17},{10,2},{18,10},{26,18},{... | collective-permute-start | bytes 387080 | tf_op jit(solution)/shard_map/ppermute | solution.py:23
  264.4 113.6 %collective-permute-start.14 = (f32[56,9,64]{2,0,1:T(8,128)S(1)}, f32[56,9,64]{2,0,1:T(8,128)S(1)}, u32[]{:S(2)}, u32[]{:S(2)}) collective-permute-start(f32[56,9,64]{2,0,1:T(8,128)S(1)} %get-tuple-element.753), channel_id=1, source_target_pairs={{0,8},{8,16},{16,24},{1,9},{9,17},{17,25},{2,10},{10,18},{18,26},{... | collective-permute-start | bytes 387080 | tf_op jit(solution)/shard_map/ppermute | solution.py:23
  267.5 110.5 %collective-permute-start.13 = (f32[56,9,64]{2,0,1:T(8,128)S(1)}, f32[56,9,64]{2,0,1:T(8,128)S(1)}, u32[]{:S(2)}, u32[]{:S(2)}) collective-permute-start(f32[56,9,64]{2,0,1:T(8,128)S(1)} %get-tuple-element.754), channel_id=1, source_target_pairs={{0,5},{1,6},{2,7},{3,0},{4,1},{5,2},{6,3},{7,4},{8,13},{9,14},{10,... | collective-permute-start | bytes 387080 | tf_op jit(solution)/shard_map/ppermute | solution.py:17
  328.0 50.0 %collective-permute-start.12 = (f32[56,9,64]{2,0,1:T(8,128)S(1)}, f32[56,9,64]{2,0,1:T(8,128)S(1)}, u32[]{:S(2)}, u32[]{:S(2)}) collective-permute-start(f32[56,9,64]{2,0,1:T(8,128)S(1)} %get-tuple-element.755), channel_id=1, source_target_pairs={{0,6},{1,7},{2,0},{3,1},{4,2},{5,3},{6,4},{7,5},{8,14},{9,15},{10,... | collective-permute-start | bytes 387080 | tf_op jit(solution)/shard_map/ppermute | solution.py:17
  328.3 18.3 %collective-permute-start.8 = (f32[56,9,64]{2,0,1:T(8,128)S(1)}, f32[56,9,64]{2,0,1:T(8,128)S(1)}, u32[]{:S(2)}, u32[]{:S(2)}) collective-permute-start(f32[56,9,64]{2,0,1:T(8,128)S(1)} %get-tuple-element.759), channel_id=1, source_target_pairs={{0,1},{1,2},{2,3},{3,4},{4,5},{5,6},{6,7},{7,0},{8,9},{9,10},{10,1... | collective-permute-start | bytes 387080 | tf_op jit(solution)/shard_map/ppermute | solution.py:17
  346.6 10.0 %collective-permute-start.9 = (f32[56,9,64]{2,0,1:T(8,128)S(1)}, f32[56,9,64]{2,0,1:T(8,128)S(1)}, u32[]{:S(2)}, u32[]{:S(2)}) collective-permute-start(f32[56,9,64]{2,0,1:T(8,128)S(1)} %get-tuple-element.758), channel_id=1, source_target_pairs={{0,2},{1,3},{2,4},{3,5},{4,6},{5,7},{6,0},{7,1},{8,10},{9,11},{10,... | collective-permute-start | bytes 387080 | tf_op jit(solution)/shard_map/ppermute | solution.py:17
  356.6 13.0 %collective-permute-start.10 = (f32[56,9,64]{2,0,1:T(8,128)S(1)}, f32[56,9,64]{2,0,1:T(8,128)S(1)}, u32[]{:S(2)}, u32[]{:S(2)}) collective-permute-start(f32[56,9,64]{2,0,1:T(8,128)S(1)} %get-tuple-element.757), channel_id=1, source_target_pairs={{0,3},{1,4},{2,5},{3,6},{4,7},{5,0},{6,1},{7,2},{8,11},{9,12},{10,... | collective-permute-start | bytes 387080 | tf_op jit(solution)/shard_map/ppermute | solution.py:17
  369.6 8.3 %collective-permute-start.11 = (f32[56,9,64]{2,0,1:T(8,128)S(1)}, f32[56,9,64]{2,0,1:T(8,128)S(1)}, u32[]{:S(2)}, u32[]{:S(2)}) collective-permute-start(f32[56,9,64]{2,0,1:T(8,128)S(1)} %get-tuple-element.756), channel_id=1, source_target_pairs={{0,7},{1,0},{2,1},{3,2},{4,3},{5,4},{6,5},{7,6},{8,15},{9,8},{10,9... | collective-permute-start | bytes 387080 | tf_op jit(solution)/shard_map/ppermute | solution.py:17
  501.2 67.6 %collective-permute-start.16 = (f32[56,9,64]{2,0,1:T(8,128)S(1)}, f32[56,9,64]{2,0,1:T(8,128)S(1)}, u32[]{:S(2)}, u32[]{:S(2)}) collective-permute-start(f32[56,9,64]{2,0,1:T(8,128)S(1)} %get-tuple-element.751), channel_id=1, source_target_pairs={{0,1},{1,2},{2,3},{3,4},{4,5},{5,6},{6,7},{7,0},{8,9},{9,10},{10,1... | collective-permute-start | bytes 387080 | tf_op jit(solution)/shard_map/ppermute | solution.py:17
  502.5 106.7 %collective-permute-start.23 = (f32[56,9,64]{2,0,1:T(8,128)S(1)}, f32[56,9,64]{2,0,1:T(8,128)S(1)}, u32[]{:S(2)}, u32[]{:S(2)}) collective-permute-start(f32[56,9,64]{2,0,1:T(8,128)S(1)} %get-tuple-element.744), channel_id=1, source_target_pairs={{8,0},{16,8},{24,16},{9,1},{17,9},{25,17},{10,2},{18,10},{26,18},{... | collective-permute-start | bytes 387080 | tf_op jit(solution)/shard_map/ppermute | solution.py:23
  503.7 105.4 %collective-permute-start.22 = (f32[56,9,64]{2,0,1:T(8,128)S(1)}, f32[56,9,64]{2,0,1:T(8,128)S(1)}, u32[]{:S(2)}, u32[]{:S(2)}) collective-permute-start(f32[56,9,64]{2,0,1:T(8,128)S(1)} %get-tuple-element.745), channel_id=1, source_target_pairs={{0,8},{8,16},{16,24},{1,9},{9,17},{17,25},{2,10},{10,18},{18,26},{... | collective-permute-start | bytes 387080 | tf_op jit(solution)/shard_map/ppermute | solution.py:23
  506.8 102.3 %collective-permute-start.21 = (f32[56,9,64]{2,0,1:T(8,128)S(1)}, f32[56,9,64]{2,0,1:T(8,128)S(1)}, u32[]{:S(2)}, u32[]{:S(2)}) collective-permute-start(f32[56,9,64]{2,0,1:T(8,128)S(1)} %get-tuple-element.746), channel_id=1, source_target_pairs={{0,5},{1,6},{2,7},{3,0},{4,1},{5,2},{6,3},{7,4},{8,13},{9,14},{10,... | collective-permute-start | bytes 387080 | tf_op jit(solution)/shard_map/ppermute | solution.py:17
  568.4 40.6 %collective-permute-start.20 = (f32[56,9,64]{2,0,1:T(8,128)S(1)}, f32[56,9,64]{2,0,1:T(8,128)S(1)}, u32[]{:S(2)}, u32[]{:S(2)}) collective-permute-start(f32[56,9,64]{2,0,1:T(8,128)S(1)} %get-tuple-element.747), channel_id=1, source_target_pairs={{0,6},{1,7},{2,0},{3,1},{4,2},{5,3},{6,4},{7,5},{8,14},{9,15},{10,... | collective-permute-start | bytes 387080 | tf_op jit(solution)/shard_map/ppermute | solution.py:17
  568.8 17.7 %collective-permute-start.17 = (f32[56,9,64]{2,0,1:T(8,128)S(1)}, f32[56,9,64]{2,0,1:T(8,128)S(1)}, u32[]{:S(2)}, u32[]{:S(2)}) collective-permute-start(f32[56,9,64]{2,0,1:T(8,128)S(1)} %get-tuple-element.750), channel_id=1, source_target_pairs={{0,2},{1,3},{2,4},{3,5},{4,6},{5,7},{6,0},{7,1},{8,10},{9,11},{10,... | collective-permute-start | bytes 387080 | tf_op jit(solution)/shard_map/ppermute | solution.py:17
  586.5 15.3 %collective-permute-start.18 = (f32[56,9,64]{2,0,1:T(8,128)S(1)}, f32[56,9,64]{2,0,1:T(8,128)S(1)}, u32[]{:S(2)}, u32[]{:S(2)}) collective-permute-start(f32[56,9,64]{2,0,1:T(8,128)S(1)} %get-tuple-element.749), channel_id=1, source_target_pairs={{0,3},{1,4},{2,5},{3,6},{4,7},{5,0},{6,1},{7,2},{8,11},{9,12},{10,... | collective-permute-start | bytes 387080 | tf_op jit(solution)/shard_map/ppermute | solution.py:17
  601.9 7.2 collective-permute-start.19
  (189 other events, 1376.0 us)
Sparse Core Ops, SparseCore 0:
  741.3 58.3 reduce-scatter.3
